TPU v7x, 32 devices: a whole 2x2x4 slice. The times are simulated.
32 devices in a mesh: dp: 8 (over z, x), parity: 4 (over y, core).
Axes of the slice: x: 2, y: 2, z: 4, core: 2. Of those that a mesh axis runs over, the one named last changes fastest.
Arguments:
- first_moment: float32 [16384, 512], P(('dp', 'parity')), may hold values from -6 to 6
- second_moment: float32 [16384, 512], P(('dp', 'parity')), may hold values from 0.01 to 4
- new_owner: int32 [16384, 1], P(('dp', 'parity')), may hold values from 0 to 7; in each aligned block of 512 rows (0 to 511, 512 to 1023, ...) at most 80 rows name the same one
- code_index: int32 [2, 4], replicated, may hold values from 0 to 7
Outputs:
- new_first: float32 [20480, 512], P(('dp', 'parity'))
- new_second: float32 [20480, 512], P(('dp', 'parity'))
- parity: float32 [5120, 2048], P(('dp', 'parity'))
- loads: int32 [8, 4], P('dp', 'parity')
Inputs may be any that keep to these rules, and one draw needn't show every extreme that they name: `new_owner`: in the rows of one device (aligned blocks of 512 rows) no owner is named more than 80 times, a bound that some owner reaches in some blocks.
All inputs are finite; a program needn't handle non-finite values.
Results may differ from a plain program's by a relative error of at most 0.0003.
Values sent between devices are 32-bit elements; how exact they have to be, the bound alone decides.
A program may use at most 64 MiB of HBM per device.

v0:
```python
import jax
import jax.numpy as jnp
from jax import lax
from jax.sharding import PartitionSpec as P


def body(first_moment, second_moment, new_owner, code_index):
    held = first_moment.shape[0]
    width = first_moment.shape[1]
    owners_count = lax.axis_size("dp")
    members = lax.axis_size("parity")
    room = held // owners_count + max(1, held // (4 * owners_count))
    capacity = owners_count * room
    owner = new_owner[:, 0]
    onehot = (owner[:, None] == jnp.arange(owners_count, dtype=jnp.int32)[None, :]).astype(
        jnp.int32
    )
    before = jnp.cumsum(onehot, axis=0) - onehot
    rank = jnp.sum(before * onehot, axis=1)
    target = owner * room + rank
    send_first = jnp.zeros((capacity, width), jnp.float32).at[target].set(first_moment)
    send_second = jnp.zeros((capacity, width), jnp.float32).at[target].set(second_moment)
    counts = jnp.sum(onehot, axis=0)
    got_first, got_second = (
        lax.all_to_all(send_first, "dp", split_axis=0, concat_axis=0, tiled=True),
        lax.all_to_all(send_second, "dp", split_axis=0, concat_axis=0, tiled=True),
    )
    totals = lax.psum(counts, "dp")
    mine = lax.dynamic_slice_in_dim(totals, lax.axis_index("dp"), 1, 0)
    loads = jnp.reshape(mine, (1, 1))
    coef = code_index.astype(jnp.float32) * 0.25
    units = coef.shape[0]
    rows = capacity // members
    share_first, share_second = (
        lax.all_to_all(got_first, "parity", split_axis=0, concat_axis=0, tiled=True),
        lax.all_to_all(got_second, "parity", split_axis=0, concat_axis=0, tiled=True),
    )
    joined = jnp.concatenate(
        [share_first.reshape(members, rows, width), share_second.reshape(members, rows, width)],
        axis=2,
    )
    parity = jnp.einsum("rp,psc->src", coef, joined, precision=lax.Precision.HIGHEST)
    parity = parity.reshape(rows, units * 2 * width)
    return (got_first, got_second, parity, loads)


def solution(mesh):
    return jax.shard_map(
        body,
        mesh=mesh,
        in_specs=(
            P(("dp", "parity"), None),
            P(("dp", "parity"), None),
            P(("dp", "parity"), None),
            P(),
        ),
        out_specs=(
            P(("dp", "parity"), None),
            P(("dp", "parity"), None),
            P(("dp", "parity"), None),
            P("dp", "parity"),
        ),
        check_vma=False,
    )
```

profile of v0, /device:TPU:0, one launch (start us, length us, event | category | flops | bytes accessed | tf_op | source)
XLA Modules:
  0.0 135.1 jit_solution(7760893199892556803)
XLA Ops:
  0.6 0.7 fusion.10
  1.3 1.1 reduce-window.6
  2.4 0.2 slice_reduce_fusion
  2.7 0.9 convert_reduce_fusion
  3.6 0.7 compare_select_fusion
  4.3 4.0 %scatter_custom_fusion.1 = f32[640,512]{1,0:T(8,128)} fusion(s32[512]{0:T(512)S(1)} %bitcast.31, f32[512,512]{1,0:T(8,128)} %param.5, f32[]{:T(128)} %constant.8.clone.1), kind=kCustom, calls=%fused_computation.6 | custom fusion | bytes 1311232 | tf_op jit(solution)/shard_map/scatter | solution.py:22
  8.3 7.3 %all-to-all-start.1 = ((f32[8,80,512]{2,1,0:T(8,128)}), f32[8,80,512]{2,1,0:T(8,128)S(1)}, u32[]{:S(2)}, u32[]{:S(2)}) async-start(f32[8,80,512]{2,1,0:T(8,128)} %bitcast.8), calls=%async_computation.1 | async-start | bytes 2621440 | tf_op jit(solution)/shard_map/all_to_all | solution.py:26
  15.6 3.2 %scatter_custom_fusion = f32[640,512]{1,0:T(8,128)S(1)} fusion(s32[512]{0:T(512)S(1)} %bitcast.32, f32[512,512]{1,0:T(8,128)} %param.4, f32[]{:T(128)} %constant.8.clone.1), kind=kCustom, calls=%fused_computation.8 | custom fusion | bytes 1311232 | tf_op jit(solution)/shard_map/scatter | solution.py:21
  18.8 28.1 %all-to-all-done.1 = f32[8,80,512]{2,1,0:T(8,128)S(1)} async-done(((f32[8,80,512]{2,1,0:T(8,128)}), f32[8,80,512]{2,1,0:T(8,128)S(1)}, u32[]{:S(2)}, u32[]{:S(2)}) %all-to-all-start.1) | async-done | bytes 1310752 | tf_op jit(solution)/shard_map/all_to_all | solution.py:26
  46.9 35.0 %all_to_all.42 = f32[8,80,512]{2,1,0:T(8,128)} all-to-all(f32[8,80,512]{2,1,0:T(8,128)S(1)} %bitcast.25), channel_id=1, replica_groups=mesh['dp'=8,'parity'=4] {'dp'}, dimensions={0} | all-to-all | bytes 2621440 | tf_op jit(solution)/shard_map/all_to_all | solution.py:25
  82.0 20.4 %all_to_all.43 = f32[4,160,512]{2,1,0:T(8,128)} all-to-all(f32[4,160,512]{2,1,0:T(8,128)S(1)} %bitcast.23), channel_id=1, replica_groups=mesh['dp'=8,'parity'=4] {'parity'}, dimensions={0} | all-to-all | bytes 2621440 | tf_op jit(solution)/shard_map/all_to_all | solution.py:36
  102.4 3.5 %all-to-all-start.2 = ((f32[4,160,512]{2,1,0:T(8,128)}), f32[4,160,512]{2,1,0:T(8,128)S(1)}, u32[]{:S(2)}, u32[]{:S(2)}) async-start(f32[4,160,512]{2,1,0:T(8,128)} %bitcast.10), calls=%async_computation.2 | async-start | bytes 2621440 | tf_op jit(solution)/shard_map/all_to_all | solution.py:35
  106.0 9.2 %psum.7 = s32[8]{0:T(128)S(1)} all-reduce(s32[8]{0:T(128)S(1)} %get-tuple-element.4), channel_id=1, replica_groups=mesh['dp'=8,'parity'=4] {'dp'}, use_global_device_ids=true, to_apply=%region_6.7 | all-reduce | flops 8 | bytes 64 | tf_op jit(solution)/shard_map/psum | solution.py:28
  115.2 0.6 dynamic_slice.3
  115.8 3.2 %copy.11 = f32[4,160,512]{2,0,1:T(4,128)} copy(f32[4,160,512]{2,1,0:T(8,128)} %all_to_all.43) | data formatting | bytes 2621440 | tf_op jit(solution)/shard_map/all_to_all | solution.py:36
  119.0 0.0 copy-start.1
  119.0 4.2 %all-to-all-done.2 = f32[4,160,512]{2,1,0:T(8,128)S(1)} async-done(((f32[4,160,512]{2,1,0:T(8,128)}), f32[4,160,512]{2,1,0:T(8,128)S(1)}, u32[]{:S(2)}, u32[]{:S(2)}) %all-to-all-start.2) | async-done | bytes 1310752 | tf_op jit(solution)/shard_map/all_to_all | solution.py:35
  123.2 0.0 copy-start
  123.2 0.8 copy.10
  124.0 0.0 copy-done.1
  124.0 0.5 copy-done
  124.5 5.6 %fusion = f32[160,1024,2]{1,2,0:T(2,128)S(1)} fusion(f32[4,160,512]{2,0,1:T(4,128)S(1)} %copy-done, f32[4,160,512]{2,0,1:T(4,128)S(1)} %copy.10, s32[2,4]{1,0:T(2,128)S(1)} %copy-done.1), kind=kOutput, calls=%fused_computation.2 | convolution fusion | flops 16384016 | bytes 3932192 | tf_op jit(solution)/shard_map/rp,psc->src/dot_general | solution.py:42
  130.0 1.5 %copy.12 = f32[20,8,2,1024]{3,1,2,0:T(8,128)} copy(f32[20,8,2,1024]{3,2,1,0:T(2,128)S(1)} %bitcast.26) | data formatting | bytes 2621440
  131.6 2.5 %copy.15 = f32[640,512]{1,0:T(8,128)} copy(f32[640,512]{1,0:T(8,128)} %bitcast.7) | data formatting | bytes 2621440
  134.0 1.1 copy.16
  (2 shorter events, 0.0 us)
Async XLA Ops:
  8.3 38.7 %all-to-all-start.1 = ((f32[8,80,512]{2,1,0:T(8,128)}), f32[8,80,512]{2,1,0:T(8,128)S(1)}, u32[]{:S(2)}, u32[]{:S(2)}) async-start(f32[8,80,512]{2,1,0:T(8,128)} %bitcast.8), calls=%async_computation.1 | async-start | bytes 2621440 | tf_op jit(solution)/shard_map/all_to_all | solution.py:26
  102.4 20.8 %all-to-all-start.2 = ((f32[4,160,512]{2,1,0:T(8,128)}), f32[4,160,512]{2,1,0:T(8,128)S(1)}, u32[]{:S(2)}, u32[]{:S(2)}) async-start(f32[4,160,512]{2,1,0:T(8,128)} %bitcast.10), calls=%async_computation.2 | async-start | bytes 2621440 | tf_op jit(solution)/shard_map/all_to_all | solution.py:35
  119.0 5.0 %copy-start.1 = (s32[2,4]{1,0:T(2,128)S(1)}, s32[2,4]{1,0:T(2,128)}, u32[]{:S(2)}) copy-start(s32[2,4]{1,0:T(2,128)} %param.7) | copy-start | bytes 100
  123.2 1.3 copy-start
where the time goes:
time: 136 us; the launch traced here: 135 us
  blocking collectives  64.7 us (48%)
  waiting for transfers between devices  32.3 us (24%)
  local copies, waits for them, and re-layouts  17.6 us (13%)
  starting transfers between devices  10.8 us (8%)
  matrix products  5.55 us (4%)
  other arithmetic  3.42 us (3%)
    all_to_all x1, blocking collectives, body(): lax.all_to_all(send_first, 'dp', split_axis=0, concat_axis=0, tiled=True)  35 us
    all_to_all x1, waiting for transfers between devices, body(): lax.all_to_all(send_second, 'dp', split_axis=0, concat_axis=0, tiled=True)  28.1 us
    all_to_all x1, blocking collectives, body(): lax.all_to_all(got_second, 'parity', split_axis=0, concat_axis=0, tiled=T...  20.4 us
    psum x1, blocking collectives, body(): totals = lax.psum(counts, 'dp')  9.21 us
    all_to_all x1, starting transfers between devices, body(): lax.all_to_all(send_second, 'dp', split_axis=0, concat_axis=0, tiled=True)  7.28 us
    dot_general x1, matrix products, body(): jnp.einsum('rp,psc->src', coef, joined, precision=lax.Precision.HIGHEST)  5.55 us
    unnamed x7, local copies, waits for them, and re-layouts  5.51 us
    all_to_all x1, waiting for transfers between devices, body(): lax.all_to_all(got_first, 'parity', split_axis=0, concat_axis=0, tiled=True)  4.19 us
  transfers between devices with their start and end apart: 2, of which 2 were waited for; matrix products, arithmetic and copies ran while one was open for 5% of the time, Pallas kernels for 0%

commit v1 on v0

v1 whole, which is shorter than its diff:
```python
import functools

import jax
import jax.numpy as jnp
from jax import lax
from jax.experimental import pallas as pl
from jax.experimental.pallas import tpu as pltpu
from jax.sharding import PartitionSpec as P

MESH = pl.DeviceIdType.MESH


def partner(me, step, n):
    if n & (n - 1):
        return lax.rem(step + n - me, n)
    other, bit = me, 1
    while bit < n:
        if step & bit:
            other = other + bit * (1 - 2 * lax.rem(me // bit, 2))
        bit *= 2
    return other


def kernel(
    n,
    members,
    room,
    slots,
    x_first,
    x_second,
    owner_ref,
    code_ref,
    got_first,
    got_second,
    mixed,
    loads_ref,
    send_first,
    send_second,
    stripe,
    count_send,
    count_got,
    send_sem,
    recv_sem,
    pass_sem,
    land_sem,
    count_send_sem,
    count_recv_sem,
):
    me = lax.axis_index("dp")
    col = lax.axis_index("parity")
    held, width = x_first.shape
    per = n // members
    units = code_ref.shape[0]

    barrier = pltpu.get_barrier_semaphore()
    for step in range(n):
        other = partner(me, step, n)

        @pl.when(other != me)
        def _():
            pl.semaphore_signal(barrier, inc=1, device_id=(other, col), device_id_type=MESH)

    for off in range(1, members):
        pl.semaphore_signal(
            barrier, inc=1, device_id=(me, lax.rem(col + off, members)), device_id_type=MESH
        )

    owner = owner_ref[...]
    names = lax.broadcasted_iota(jnp.int32, (n, held), 0)
    hot = owner == names
    earlier = lax.broadcasted_iota(jnp.int32, (held, held), 0) < lax.broadcasted_iota(
        jnp.int32, (held, held), 1
    )
    before = jnp.dot(
        hot.astype(jnp.bfloat16), earlier.astype(jnp.bfloat16), preferred_element_type=jnp.float32
    )
    rank = jnp.sum(jnp.where(hot, before, 0.0), axis=0, keepdims=True).astype(jnp.int32)
    target = owner * slots + rank
    count = jnp.sum(hot.astype(jnp.int32), axis=1, keepdims=True)
    count_send[...] = jnp.broadcast_to(count, count_send.shape)
    place = (target == lax.broadcasted_iota(jnp.int32, (n * slots, held), 0)).astype(jnp.bfloat16)

    def pack(x_ref, send_ref):
        x = x_ref[...]
        high = x.astype(jnp.bfloat16)
        rest = x - high.astype(jnp.float32)
        mid = rest.astype(jnp.bfloat16)
        low = (rest - mid.astype(jnp.float32)).astype(jnp.bfloat16)
        total = jnp.dot(place, low, preferred_element_type=jnp.float32)
        total += jnp.dot(place, mid, preferred_element_type=jnp.float32)
        total += jnp.dot(place, high, preferred_element_type=jnp.float32)
        send_ref[...] = total

    def rows(index):
        return pl.ds(pl.multiple_of(index * slots, 8), slots)

    sends = ((x_first, send_first, got_first), (x_second, send_second, got_second))

    def exchange(m, step, other):
        return pltpu.make_async_remote_copy(
            src_ref=sends[m][1].at[rows(other)],
            dst_ref=sends[m][2].at[rows(me)],
            send_sem=send_sem.at[m, step],
            recv_sem=recv_sem.at[m, step],
            device_id=(other, col),
            device_id_type=MESH,
        )

    def arrival(m, step, other):
        return pltpu.make_async_remote_copy(
            src_ref=sends[m][1].at[rows(other)],
            dst_ref=sends[m][2].at[rows(other)],
            send_sem=send_sem.at[m, step],
            recv_sem=recv_sem.at[m, step],
            device_id=(other, col),
            device_id_type=MESH,
        )

    def counted(step, other):
        return pltpu.make_async_remote_copy(
            src_ref=count_send,
            dst_ref=count_got.at[step],
            send_sem=count_send_sem.at[step],
            recv_sem=count_recv_sem.at[step],
            device_id=(other, col),
            device_id_type=MESH,
        )

    for m in range(2):
        pack(sends[m][0], sends[m][1])
        if m == 0:
            pl.semaphore_wait(barrier, n - 1 + members - 1)
        for step in range(1, n):
            other = partner(me, step, n)
            exchange(m, step, other).start()
    for step in range(1, n):
        counted(step, partner(me, step, n)).start()

    def onward(m, step, origin, src):
        keeper, place_in = origin // per, lax.rem(origin, per)
        return keeper, pltpu.make_async_remote_copy(
            src_ref=src.at[rows(origin)],
            dst_ref=stripe.at[col, place_in, m],
            send_sem=pass_sem.at[m, step],
            recv_sem=land_sem.at[col, place_in, m],
            device_id=(me, keeper),
            device_id_type=MESH,
        )

    for m in range(2):
        got = sends[m][2]
        got[rows(me), :] = sends[m][1][rows(me), :]

    for m in range(2):
        for step in range(n):
            origin = partner(me, step, n)
            src = sends[m][1] if step == 0 else sends[m][2]
            if step > 0:
                arrival(m, step, origin).wait_recv()
            keeper, copy = onward(m, step, origin, src)

            @pl.when(keeper != col)
            def _():
                copy.start()

    total = count_send[...]
    for step in range(1, n):
        counted(step, partner(me, step, n)).wait_recv()
        total = total + count_got[step]
    mine = lax.broadcasted_iota(jnp.int32, total.shape, 0) == me
    loads_ref[...] = jnp.sum(jnp.where(mine, total, 0), axis=0, keepdims=True)[:, :1]

    for m in range(2):
        for u in range(per):
            origin = col * per + u
            weight = [code_ref[r, col].astype(jnp.float32) * 0.25 for r in range(units)]
            block = sends[m][2][rows(origin), :]
            acc = [block * weight[r] for r in range(units)]
            for off in range(1, members):
                other = lax.rem(col + off, members)
                pltpu.make_async_remote_copy(
                    src_ref=stripe.at[other, u, m],
                    dst_ref=stripe.at[other, u, m],
                    send_sem=pass_sem.at[m, 0],
                    recv_sem=land_sem.at[other, u, m],
                    device_id=(me, other),
                    device_id_type=MESH,
                ).wait_recv()
                block = stripe[other, u, m]
                for r in range(units):
                    acc[r] = acc[r] + block * (code_ref[r, other].astype(jnp.float32) * 0.25)
            for r in range(units):
                mixed[u * slots:(u + 1) * slots, (2 * r + m) * width:(2 * r + m + 1) * width] = acc[r]

    for m in range(2):
        for step in range(n):
            origin = partner(me, step, n)
            src = sends[m][1] if step == 0 else sends[m][2]
            if step > 0:
                exchange(m, step, origin).wait_send()
            keeper, copy = onward(m, step, origin, src)

            @pl.when(keeper != col)
            def _():
                copy.wait_send()
    for step in range(1, n):
        counted(step, partner(me, step, n)).wait_send()


def body(first_moment, second_moment, new_owner, code_index):
    held, width = first_moment.shape
    n = lax.axis_size("dp")
    members = lax.axis_size("parity")
    room = held // n + max(1, held // (4 * n))
    slots = -(-room // 8) * 8
    per = n // members
    units = code_index.shape[0]
    f32 = jnp.float32
    vmem = pl.BlockSpec(memory_space=pltpu.VMEM)
    dma = pltpu.SemaphoreType.DMA
    new_first, new_second, parity, loads = pl.pallas_call(
        functools.partial(kernel, n, members, room, slots),
        out_shape=(
            jax.ShapeDtypeStruct((n * slots, width), f32),
            jax.ShapeDtypeStruct((n * slots, width), f32),
            jax.ShapeDtypeStruct((per * slots, units * 2 * width), f32),
            jax.ShapeDtypeStruct((1, 1), jnp.int32),
        ),
        in_specs=[vmem, vmem, vmem, pl.BlockSpec(memory_space=pltpu.SMEM)],
        out_specs=(vmem, vmem, vmem, vmem),
        scratch_shapes=[
            pltpu.VMEM((n * slots, width), f32),
            pltpu.VMEM((n * slots, width), f32),
            pltpu.VMEM((members, per, 2, slots, width), f32),
            pltpu.VMEM((n, 128), jnp.int32),
            pltpu.VMEM((n, n, 128), jnp.int32),
            dma((2, n)),
            dma((2, n)),
            dma((2, n)),
            dma((members, per, 2)),
            dma((n,)),
            dma((n,)),
        ],
        compiler_params=pltpu.CompilerParams(
            collective_id=0, has_side_effects=True, vmem_limit_bytes=48 * 1024 * 1024
        ),
    )(first_moment, second_moment, new_owner.reshape(1, held), code_index)
    if slots != room:
        new_first, new_second = (
            a.reshape(n, slots, width)[:, :room].reshape(n * room, width)
            for a in (new_first, new_second)
        )
        parity = parity.reshape(per, slots, -1)[:, :room].reshape(per * room, -1)
    return new_first, new_second, parity, loads


def solution(mesh):
    return jax.shard_map(
        body,
        mesh=mesh,
        in_specs=(
            P(("dp", "parity"), None),
            P(("dp", "parity"), None),
            P(("dp", "parity"), None),
            P(),
        ),
        out_specs=(
            P(("dp", "parity"), None),
            P(("dp", "parity"), None),
            P(("dp", "parity"), None),
            P("dp", "parity"),
        ),
        check_vma=False,
    )
```

time: 136 us -> 80.2 us (0.59)
  Pallas kernels: 0 us -> 70.6 us
  blocking collectives: 64.7 us -> 0 us
  waiting for transfers between devices: 32.3 us -> 0 us
  starting transfers between devices: 10.8 us -> 0 us
  local copies, waits for them, and re-layouts: 17.6 us -> 6.97 us
  matrix products: 5.55 us -> 0 us
  other arithmetic: 3.42 us -> 0 us
  between operations: 0.68 us -> 2.4 us
    pallas_call x0 -> x1, Pallas kernels: none -> 70.6 us  [body(): pl.pallas_call(functools.partial(kernel, n, members, room, slots), out_sh...]
    all_to_all x2 -> x0, blocking collectives: 55.5 us -> none  [the longest x1 35 us: body(): lax.all_to_all(send_first, 'dp', split_axis=0, concat_axis=0, tiled=True)]
    all_to_all x2 -> x0, waiting for transfers between devices: 32.3 us -> none  [the longest x1 28.1 us: body(): lax.all_to_all(send_second, 'dp', split_axis=0, concat_axis=0, tiled=True)]
    all_to_all x2 -> x0, starting transfers between devices: 10.8 us -> none  [the longest x1 7.28 us: body(): lax.all_to_all(send_second, 'dp', split_axis=0, concat_axis=0, tiled=True)]
    psum x1 -> x0, blocking collectives: 9.21 us -> none  [body(): totals = lax.psum(counts, 'dp')]
    scatter x2 -> x0, local copies, waits for them, and re-layouts: 7.24 us -> none  [the longest x1 4 us: body(): jnp.zeros((capacity, width), jnp.float32).at[target].set(second_moment)]
    dot_general x1 -> x0, matrix products: 5.55 us -> none  [body(): jnp.einsum('rp,psc->src', coef, joined, precision=lax.Precision.HIGHEST)]
    all_to_all x2 -> x0, local copies, waits for them, and re-layouts: 4.06 us -> none  [the longest x1 3.22 us: body(): lax.all_to_all(got_second, 'parity', split_axis=0, concat_axis=0, tiled=T...]
  transfers between devices with their start and end apart: 2 -> 0, of which waited for: 2 -> 0; matrix products, arithmetic and copies ran while one was open for 5% -> 0% of each run, Pallas kernels for 0% -> 0%
where the time goes in v1:
time: 80.2 us; the launch traced here: 79.9 us
  Pallas kernels  70.6 us (88%)
  local copies, waits for them, and re-layouts  6.97 us (9%)
  between operations  2.4 us (3%)
    pallas_call x1, Pallas kernels, body(): pl.pallas_call(functools.partial(kernel, n, members, room, slots), out_sh...  70.6 us
    unnamed x11, local copies, waits for them, and re-layouts  6.97 us

profile of v1, /device:TPU:0, one launch (start us, length us, event | category | flops | bytes accessed | tf_op | source)
XLA Modules:
  0.0 79.9 jit_solution(15402548728529942455)
XLA Ops:
  0.6 0.0 copy-start
  0.6 1.2 %copy-done = f32[512,512]{1,0:T(8,128)S(1)} copy-done((f32[512,512]{1,0:T(8,128)S(1)}, f32[512,512]{1,0:T(8,128)}, u32[]{:S(2)}) %copy-start) | copy-done | bytes 1048600
  1.9 0.0 copy-start.1
  1.9 1.2 %copy-done.1 = f32[512,512]{1,0:T(8,128)S(1)} copy-done((f32[512,512]{1,0:T(8,128)S(1)}, f32[512,512]{1,0:T(8,128)}, u32[]{:S(2)}) %copy-start.1) | copy-done | bytes 1048600
  3.1 0.0 copy-start.2
  3.1 0.7 copy-done.2
  3.8 0.0 copy-start.3
  3.8 0.7 copy-done.3
  4.4 70.6 %shard_map.75 = (f32[640,512]{1,0:T(8,128)S(1)}, f32[640,512]{1,0:T(8,128)S(1)}, f32[160,2048]{1,0:T(8,128)S(1)}, s32[1,1]{1,0:T(1,128)}) custom-call(f32[512,512]{1,0:T(8,128)S(1)} %copy-done, f32[512,512]{1,0:T(8,128)S(1)} %copy-done.1, s32[1,512]{1,0:T(1,128)S(1)} %bitcast.1, s32[2,4]{1,0:T(2,128)S(1)} %copy-done.3), custom_call_target="tpu_custom_call" | custom-call | tf_op jit(solution)/shard_map/pallas_call | solution.py:221
  75.0 1.1 %copy.12 = f32[640,512]{1,0:T(8,128)} copy(f32[640,512]{1,0:T(8,128)S(1)} %get-tuple-element.8) | data formatting | bytes 2621440
  76.1 1.1 %copy.13 = f32[640,512]{1,0:T(8,128)} copy(f32[640,512]{1,0:T(8,128)S(1)} %get-tuple-element.9) | data formatting | bytes 2621440
  77.1 1.1 %copy.14 = f32[160,2048]{1,0:T(8,128)} copy(f32[160,2048]{1,0:T(8,128)S(1)} %get-tuple-element.10) | data formatting | bytes 2621440
Async XLA Ops:
  0.6 1.2 %copy-start = (f32[512,512]{1,0:T(8,128)S(1)}, f32[512,512]{1,0:T(8,128)}, u32[]{:S(2)}) copy-start(f32[512,512]{1,0:T(8,128)} %x_first.1) | copy-start | bytes 3145732
  1.9 1.2 %copy-start.1 = (f32[512,512]{1,0:T(8,128)S(1)}, f32[512,512]{1,0:T(8,128)}, u32[]{:S(2)}) copy-start(f32[512,512]{1,0:T(8,128)} %x_second.1) | copy-start | bytes 3145732
  3.1 0.7 copy-start.2
  3.8 0.7 copy-start.3

commit v2 on v1

v2 whole, which is shorter than its diff:
```python
import functools

import jax
import jax.numpy as jnp
from jax import lax
from jax.experimental import pallas as pl
from jax.experimental.pallas import tpu as pltpu
from jax.sharding import PartitionSpec as P

MESH = pl.DeviceIdType.MESH


def partner(me, step, n):
    if n & (n - 1):
        return lax.rem(step + n - me, n)
    other, bit = me, 1
    while bit < n:
        if step & bit:
            other = other + bit * (1 - 2 * lax.rem(me // bit, 2))
        bit *= 2
    return other


def exchange_kernel(
    n,
    members,
    slots,
    parts,
    first_ref,
    second_ref,
    owner_hbm,
    code_hbm,
    got_first,
    got_second,
    stripe,
    coef_ref,
    loads_ref,
    x_first,
    x_second,
    owner_ref,
    code_ref,
    send_first,
    send_second,
    count_send,
    count_got,
    in_sem,
    send_sem,
    recv_sem,
    pass_sem,
    land_sem,
    count_send_sem,
    count_recv_sem,
):
    me = lax.axis_index("dp")
    col = lax.axis_index("parity")
    held, width = x_first.shape
    per = n // members
    half = n // 2
    size = slots // parts
    units = code_hbm.shape[0]
    moments = ((x_first, send_first, got_first), (x_second, send_second, got_second))

    fetch = [
        pltpu.make_async_copy(src, dst, in_sem.at[i])
        for i, (src, dst) in enumerate(
            (
                (owner_hbm, owner_ref),
                (first_ref, x_first),
                (second_ref, x_second),
                (code_hbm, code_ref),
            )
        )
    ]
    for copy in fetch:
        copy.start()

    barrier = pltpu.get_barrier_semaphore()
    for step in range(1, n):
        pl.semaphore_signal(
            barrier, inc=1, device_id=(partner(me, step, n), col), device_id_type=MESH
        )
    for off in range(1, members):
        pl.semaphore_signal(
            barrier, inc=1, device_id=(me, lax.rem(col + off, members)), device_id_type=MESH
        )

    earlier = (
        lax.broadcasted_iota(jnp.int32, (held, held), 0)
        < lax.broadcasted_iota(jnp.int32, (held, held), 1)
    ).astype(jnp.bfloat16)
    fetch[0].wait()
    owner = owner_ref[...]
    hot = owner == lax.broadcasted_iota(jnp.int32, (n, held), 0)
    before = jnp.dot(hot.astype(jnp.bfloat16), earlier, preferred_element_type=jnp.float32)
    rank = jnp.sum(jnp.where(hot, before, 0.0), axis=0, keepdims=True).astype(jnp.int32)
    target = owner * slots + rank
    side = me // half
    bases = ((1 - side) * half, side * half)

    def pack(m, base, place):
        x = moments[m][0][...]
        high = x.astype(jnp.bfloat16)
        rest = x - high.astype(jnp.float32)
        mid = rest.astype(jnp.bfloat16)
        low = (rest - mid.astype(jnp.float32)).astype(jnp.bfloat16)
        total = jnp.dot(place, low, preferred_element_type=jnp.float32)
        total += jnp.dot(place, mid, preferred_element_type=jnp.float32)
        total += jnp.dot(place, high, preferred_element_type=jnp.float32)
        moments[m][1][pl.ds(pl.multiple_of(base * slots, 8), half * slots), :] = total

    def rows(index, part):
        return pl.ds(pl.multiple_of(index * slots + part * size, 8), size)

    def exchange(m, step, part, source):
        other = partner(me, step, n)
        return pltpu.make_async_remote_copy(
            src_ref=moments[m][1].at[rows(other, part)],
            dst_ref=moments[m][2].at[rows(source, part)],
            send_sem=send_sem.at[m, step, part],
            recv_sem=recv_sem.at[m, step, part],
            device_id=(other, col),
            device_id_type=MESH,
        )

    def counted(step):
        return pltpu.make_async_remote_copy(
            src_ref=count_send,
            dst_ref=count_got.at[step],
            send_sem=count_send_sem.at[step],
            recv_sem=count_recv_sem.at[step],
            device_id=(partner(me, step, n), col),
            device_id_type=MESH,
        )

    def onward(m, step, part):
        origin = partner(me, step, n)
        keeper = origin // per
        return keeper, pltpu.make_async_remote_copy(
            src_ref=moments[m][1 if step == 0 else 2].at[rows(origin, part)],
            dst_ref=stripe.at[m, col, rows(lax.rem(origin, per), part)],
            send_sem=pass_sem.at[m, step, part],
            recv_sem=land_sem.at[m, col, lax.rem(origin, per), part],
            device_id=(me, keeper),
            device_id_type=MESH,
        )

    far, near = range(half, n), range(1, half)
    places = []
    for base in bases:
        spots = lax.broadcasted_iota(jnp.int32, (half * slots, held), 0) + base * slots
        places.append((target == spots).astype(jnp.bfloat16))
    order = ((0, 1), (0, 0), (1, 1), (1, 0))
    for index, (m, side_of) in enumerate(order):
        if m == 0 and index == 0 or m == 1 and all(o[0] == 0 for o in order[:index]):
            fetch[1 + m].wait()
        pack(m, bases[side_of], places[side_of])
        if index == 0:
            pl.semaphore_wait(barrier, n - 1 + members - 1)
        for step in (far, near)[side_of]:
            for part in range(parts):
                exchange(m, step, part, me).start()

    count = jnp.sum(hot.astype(jnp.int32), axis=1, keepdims=True)
    count_send[...] = jnp.broadcast_to(count, count_send.shape)
    own = pl.ds(pl.multiple_of(me * slots, 8), slots)
    for m in range(2):
        moments[m][2][own, :] = moments[m][1][own, :]
    fetch[3].wait()
    for r in range(units):
        for p in range(members):
            coef_ref[r * members + p, :] = jnp.full(
                (128,), code_ref[r, p].astype(jnp.float32) * 0.25, jnp.float32
            )
    for step in range(1, n):
        counted(step).start()

    arrivals = [(m, 0) for m in range(2)]
    for m, side_of in order:
        arrivals += [(m, step) for step in (far, near)[side_of]]
    for m, step in arrivals:
        origin = partner(me, step, n)
        for part in range(parts):
            if step > 0:
                exchange(m, step, part, origin).wait_recv()
            keeper, copy = onward(m, step, part)

            @pl.when(keeper != col)
            def _():
                copy.start()

    for m in range(2):
        kept = pl.ds(pl.multiple_of(col * per * slots, 8), per * slots)
        stripe[m, col] = moments[m][2][kept, :]

    total = count_send[...]
    for step in range(1, n):
        counted(step).wait_recv()
        total = total + count_got[step]
    this = lax.broadcasted_iota(jnp.int32, total.shape, 0) == me
    loads_ref[...] = jnp.sum(jnp.where(this, total, 0), axis=0, keepdims=True)

    for m, step in arrivals:
        for part in range(parts):
            if step > 0:
                exchange(m, step, part, me).wait_send()
            keeper, copy = onward(m, step, part)

            @pl.when(keeper != col)
            def _():
                copy.wait_send()

    for step in range(1, n):
        counted(step).wait_send()

    for m in range(2):
        for off in range(1, members):
            other = lax.rem(col + off, members)
            for u in range(per):
                for part in range(parts):
                    here = stripe.at[m, other, pl.ds(u * slots + part * size, size)]
                    pltpu.make_async_remote_copy(
                        src_ref=here,
                        dst_ref=here,
                        send_sem=pass_sem.at[m, 0, part],
                        recv_sem=land_sem.at[m, other, u, part],
                        device_id=(me, other),
                        device_id_type=MESH,
                    ).wait_recv()


def finish_kernel(
    units,
    members,
    per,
    got_first,
    got_second,
    stripe,
    coef_ref,
    loads_ref,
    out_first,
    out_second,
    out_parity,
    out_loads,
    mixed,
    sem,
):
    width = got_first.shape[1]
    slots = stripe.shape[2] // per
    out = [
        pltpu.make_async_copy(got_first, out_first, sem.at[0]),
        pltpu.make_async_copy(got_second, out_second, sem.at[1]),
    ]
    for copy in out:
        copy.start()
    out_loads[...] = loads_ref[:, :1]
    for u in range(per):
        span = slice(u * slots, (u + 1) * slots)
        for m in range(2):
            for lane in range(width // 128):
                lanes = slice(lane * 128, (lane + 1) * 128)
                blocks = [stripe[m, p, span, lanes] for p in range(members)]
                for r in range(units):
                    acc = blocks[0] * coef_ref[r * members:r * members + 1, :]
                    for p in range(1, members):
                        acc += blocks[p] * coef_ref[r * members + p:r * members + p + 1, :]
                    at = (2 * r + m) * width + lane * 128
                    mixed[span, at:at + 128] = acc
        copy = pltpu.make_async_copy(mixed.at[span], out_parity.at[span], sem.at[2 + u])
        copy.start()
        out.append(copy)
    for copy in out:
        copy.wait()


def body(first_moment, second_moment, new_owner, code_index):
    held, width = first_moment.shape
    n = lax.axis_size("dp")
    members = lax.axis_size("parity")
    room = held // n + max(1, held // (4 * n))
    slots = -(-room // 8) * 8
    parts = 2 if slots % 16 == 0 else 1
    per = n // members
    units = code_index.shape[0]
    f32 = jnp.float32
    hbm = pl.BlockSpec(memory_space=pltpu.HBM)
    vmem = pl.BlockSpec(memory_space=pltpu.VMEM)
    dma = pltpu.SemaphoreType.DMA
    block = jax.ShapeDtypeStruct((n * slots, width), f32)
    got = pl.pallas_call(
        functools.partial(exchange_kernel, n, members, slots, parts),
        out_shape=(
            block,
            block,
            jax.ShapeDtypeStruct((2, members, per * slots, width), f32),
            jax.ShapeDtypeStruct((units * members, 128), f32),
            jax.ShapeDtypeStruct((1, 128), jnp.int32),
        ),
        in_specs=[hbm] * 4,
        out_specs=(vmem,) * 5,
        scratch_shapes=[
            pltpu.VMEM((held, width), f32),
            pltpu.VMEM((held, width), f32),
            pltpu.VMEM((1, held), jnp.int32),
            pltpu.SMEM(code_index.shape, jnp.int32),
            pltpu.VMEM((n * slots, width), f32),
            pltpu.VMEM((n * slots, width), f32),
            pltpu.VMEM((n, 128), jnp.int32),
            pltpu.VMEM((n, n, 128), jnp.int32),
            dma((4,)),
            dma((2, n, parts)),
            dma((2, n, parts)),
            dma((2, n, parts)),
            dma((2, members, per, parts)),
            dma((n,)),
            dma((n,)),
        ],
        compiler_params=pltpu.CompilerParams(
            collective_id=0, has_side_effects=True, vmem_limit_bytes=40 * 1024 * 1024
        ),
    )(first_moment, second_moment, new_owner.reshape(1, held), code_index)
    mixed = (per * slots, units * 2 * width)
    new_first, new_second, parity, loads = pl.pallas_call(
        functools.partial(finish_kernel, units, members, per),
        out_shape=(
            block,
            block,
            jax.ShapeDtypeStruct(mixed, f32),
            jax.ShapeDtypeStruct((1, 1), jnp.int32),
        ),
        in_specs=[vmem] * 5,
        out_specs=(hbm, hbm, hbm, vmem),
        scratch_shapes=[pltpu.VMEM(mixed, f32), dma((2 + per,))],
        compiler_params=pltpu.CompilerParams(vmem_limit_bytes=40 * 1024 * 1024),
    )(*got)
    if slots != room:
        new_first, new_second = (
            a.reshape(n, slots, width)[:, :room].reshape(n * room, width)
            for a in (new_first, new_second)
        )
        parity = parity.reshape(per, slots, -1)[:, :room].reshape(per * room, -1)
    return new_first, new_second, parity, loads


def solution(mesh):
    return jax.shard_map(
        body,
        mesh=mesh,
        in_specs=(
            P(("dp", "parity"), None),
            P(("dp", "parity"), None),
            P(("dp", "parity"), None),
            P(),
        ),
        out_specs=(
            P(("dp", "parity"), None),
            P(("dp", "parity"), None),
            P(("dp", "parity"), None),
            P("dp", "parity"),
        ),
        check_vma=False,
    )
```

time: 80.2 us -> 77.5 us (0.966)
  local copies, waits for them, and re-layouts: 6.97 us -> 3.8 us
  Pallas kernels: 70.6 us -> 72.8 us
  between operations: 2.4 us -> 0.65 us
    unnamed x11 -> x8, local copies, waits for them, and re-layouts: 6.97 us -> 3.8 us
    pallas_call x1 -> x2, Pallas kernels: 70.6 us -> 72.8 us  [the longest x1 70.3 us: body(): pl.pallas_call(functools.partial(exchange_kernel, n, members, slots, part...]
where the time goes in v2:
time: 77.5 us; the launch traced here: 77.2 us
  Pallas kernels  72.8 us (94%)
  local copies, waits for them, and re-layouts  3.8 us (5%)
    pallas_call x1, Pallas kernels, body(): pl.pallas_call(functools.partial(exchange_kernel, n, members, slots, part...  70.3 us
    unnamed x8, local copies, waits for them, and re-layouts  3.8 us
    pallas_call x1, Pallas kernels, body(): pl.pallas_call(functools.partial(finish_kernel, units, members, per), out...  2.46 us

profile of v2, /device:TPU:0, one launch (start us, length us, event | category | flops | bytes accessed | tf_op | source)
XLA Modules:
  0.0 77.2 jit_solution(11717085876636492563)
XLA Ops:
  0.6 0.0 copy-start
  0.6 1.2 %copy-done = f32[512,512]{1,0:T(8,128)S(1)} copy-done((f32[512,512]{1,0:T(8,128)S(1)}, f32[512,512]{1,0:T(8,128)}, u32[]{:S(2)}) %copy-start) | copy-done | bytes 1048600
  1.9 0.0 copy-start.1
  1.9 1.2 %copy-done.1 = f32[512,512]{1,0:T(8,128)S(1)} copy-done((f32[512,512]{1,0:T(8,128)S(1)}, f32[512,512]{1,0:T(8,128)}, u32[]{:S(2)}) %copy-start.1) | copy-done | bytes 1048600
  3.1 0.0 copy-start.2
  3.1 0.7 copy-done.2
  3.8 0.0 copy-start.3
  3.8 0.7 copy-done.3
  4.4 70.3 %shard_map.75 = (f32[640,512]{1,0:T(8,128)S(1)}, f32[640,512]{1,0:T(8,128)S(1)}, f32[2,4,160,512]{3,2,1,0:T(8,128)S(1)}, f32[8,128]{1,0:T(8,128)S(1)}, s32[1,128]{1,0:T(1,128)S(1)}) custom-call(f32[512,512]{1,0:T(8,128)S(1)} %copy-done, f32[512,512]{1,0:T(8,128)S(1)} %copy-done.1, s32[1,512]{1,0:T(1,128)S(1)} %bitcast.1, s32[2,4]{1,0:T(2,128)S(1)} %copy-done.3), custom_call_target="tpu_custom_call" | custom-call | tf_op jit(solution)/shard_map/pallas_call | solution.py:289
  74.8 2.5 %shard_map.76 = (f32[640,512]{1,0:T(8,128)}, f32[640,512]{1,0:T(8,128)}, f32[160,2048]{1,0:T(8,128)}, s32[1,1]{1,0:T(1,128)}) custom-call(f32[640,512]{1,0:T(8,128)S(1)} %get-tuple-element.9.got_first, f32[640,512]{1,0:T(8,128)S(1)} %get-tuple-element.10.got_second, f32[2,4,160,512]{3,2,1,0:T(8,128)S(1)} %get-tuple-element.11.stripe, ...), custom_call_target="tpu_custom_call" | custom-call | tf_op jit(solution)/shard_map/pallas_call | solution.py:322
Async XLA Ops:
  0.6 1.2 %copy-start = (f32[512,512]{1,0:T(8,128)S(1)}, f32[512,512]{1,0:T(8,128)}, u32[]{:S(2)}) copy-start(f32[512,512]{1,0:T(8,128)} %first_ref.1) | copy-start | bytes 3145732
  1.9 1.2 %copy-start.1 = (f32[512,512]{1,0:T(8,128)S(1)}, f32[512,512]{1,0:T(8,128)}, u32[]{:S(2)}) copy-start(f32[512,512]{1,0:T(8,128)} %second_ref.1) | copy-start | bytes 3145732
  3.1 0.7 copy-start.2
  3.8 0.7 copy-start.3
